TPU v7x, 32 devices: a whole 2x2x4 slice. The times are simulated.
32 devices in a mesh: rep: 4 (over x, core), dp: 4 (over z), tp: 2 (over y).
Axes of the slice: x: 2, y: 2, z: 4, core: 2. Of those that a mesh axis runs over, the one named last changes fastest.
Arguments:
- hidden: bfloat16 [4, 512, 14336], P('rep', None, 'tp'), may hold values from -6 to 6
- down_weight: bfloat16 [14336, 8192], P('tp', 'dp'), may hold values from -0.046875 to 0.046875
- out_grad: bfloat16 [4, 512, 8192], P('rep', 'tp', 'dp'), may hold values from -6 to 6
- pseudo_grad: bfloat16 [4, 14336, 8192], P('rep', 'tp', 'dp'), may hold values from -6 to 6
- momentum: float32 [14336, 8192], P(('tp', 'rep'), 'dp'), may hold values from -6 to 6
Outputs:
- layer_out: bfloat16 [4, 512, 8192], P('rep', 'tp', 'dp')
- hidden_grad: bfloat16 [4, 512, 14336], P('rep', 'dp', 'tp')
- new_momentum: float32 [14336, 8192], P(('tp', 'rep'), 'dp')
- outer_step: bfloat16 [14336, 8192], P('tp', 'dp')
All inputs are finite; a program needn't handle non-finite values.
Results may differ from a plain program's by a relative error of at most 0.017.
Values may be sent and summed in bfloat16 or wider, within the bound.
A program may use at most 256 MiB of HBM per device.

v0:
```python
import jax
import jax.numpy as jnp
from jax import lax
from jax.sharding import PartitionSpec as P

outer_rate = 0.7
momentum_rate = 0.9


def per_device(hidden, down_weight, out_grad, pseudo_grad, momentum):
    token_rows = hidden[0]
    local_grads = out_grad[0]
    row_block = token_rows
    layer_out = lax.psum_scatter(
        jnp.dot(row_block, down_weight, preferred_element_type=jnp.float32).astype(jnp.bfloat16),
        "tp",
        scatter_dimension=0,
        tiled=True,
    )
    all_grads = lax.all_gather(local_grads, "tp", axis=0, tiled=True)
    row_block = all_grads
    hidden_grad = lax.psum_scatter(
        lax.dot_general(
            row_block, down_weight, (((1,), (1,)), ((), ())), preferred_element_type=jnp.float32
        ).astype(jnp.bfloat16),
        "dp",
        scatter_dimension=0,
        tiled=True,
    )
    replicas = lax.axis_size("rep")
    replica_terms = pseudo_grad[0].astype(jnp.float32)
    average = (
        lax.psum_scatter(
            replica_terms.astype(jnp.bfloat16), "rep", scatter_dimension=0, tiled=True
        ).astype(jnp.float32)
        / replicas
    )
    new_momentum = momentum_rate * momentum + average
    step_share = (outer_rate * (average + momentum_rate * new_momentum)).astype(jnp.bfloat16)
    outer_step = lax.all_gather(step_share, "rep", axis=0, tiled=True)
    return (layer_out[None], hidden_grad[None], new_momentum, outer_step)


def solution(mesh):
    return jax.shard_map(
        per_device,
        mesh=mesh,
        in_specs=(
            P("rep", None, "tp"),
            P("tp", "dp"),
            P("rep", "tp", "dp"),
            P("rep", "tp", "dp"),
            P(("tp", "rep"), "dp"),
        ),
        out_specs=(
            P("rep", "tp", "dp"),
            P("rep", "dp", "tp"),
            P(("tp", "rep"), "dp"),
            P("tp", "dp"),
        ),
        check_vma=False,
    )
```

profile of v0, /device:TPU:0, one launch (start us, length us, event | category | flops | bytes accessed | tf_op | source)
XLA Modules:
  0.0 610.3 jit_solution(9170276419713844570)
XLA Ops:
  8.0 0.0 reduce-scatter.8.cloned.1.call-start
  8.0 0.7 reduce-scatter.8.cloned.1.call-update
  8.7 0.0 all-gather.6.cloned.1.call-start
  8.8 0.5 all-gather.6.cloned.1.call-update
  9.3 0.0 all-gather.4.cloned.1.call-start
  9.4 214.8 %reduce-scatter.8.cloned.1.call-done = bf16[1792,2048]{1,0:T(8,128)(2,1)} async-done(((bf16[7168,2048]{1,0:T(8,128)(2,1)}), bf16[1792,2048]{1,0:T(8,128)(2,1)}) %reduce-scatter.8.cloned.1.call-update) | async-done | bytes 7340048 | tf_op jit(solution)/shard_map/reduce_scatter | solution.py:33
  224.1 15.4 %multiply_convert_fusion = (bf16[1792,2048]{1,0:T(8,128)(2,1)}, f32[1792,2048]{1,0:T(8,128)}) fusion(bf16[1792,2048]{1,0:T(8,128)(2,1)} %reduce-scatter.8.cloned.1.call-done, f32[1792,2048]{1,0:T(8,128)} %param.9), kind=kLoop, calls=%fused_computation | loop fusion | flops 29360128 | bytes 44040192 | tf_op jit(solution)/shard_map/convert_element_type | solution.py:39
  239.5 0.0 all-gather.4.cloned.1.call-update
  239.5 0.0 reduce-scatter.4.cloned.1.call-start
  239.6 24.8 %fusion.3 = bf16[512,2048]{1,0:T(8,128)(2,1)} fusion(bf16[7168,2048]{1,0:T(8,128)(2,1)} %param.6, bf16[1,512,7168]{2,1,0:T(8,128)(2,1)} %param.5), kind=kOutput, calls=%fused_computation.6 | convolution fusion | flops 15033434112 | bytes 38797312 | tf_op jit(solution)/shard_map/dot_general | solution.py:15
  264.4 0.0 reduce-scatter.4.cloned.1.call-update
  264.4 0.0 reduce-scatter.6.cloned.1.call-start
  264.5 0.0 all-gather.6.cloned.1.call-done
  264.5 23.1 %convolution_convert_fusion = bf16[512,7168]{1,0:T(8,128)(2,1)} fusion(bf16[7168,2048]{1,0:T(8,128)(2,1)} %param.6, bf16[1,512,2048]{2,1,0:T(8,128)(2,1)} %all-gather.6.cloned.1.call-done), kind=kOutput, calls=%fused_computation.3 | convolution fusion | flops 15036055552 | bytes 38797312 | tf_op jit(solution)/shard_map/dot_general | solution.py:23
  287.6 0.0 reduce-scatter.6.cloned.1.call-update
  287.6 129.9 %all-gather.4.cloned.1.call-done = bf16[7168,2048]{1,0:T(8,128)(2,1)} async-done(((bf16[1792,2048]{1,0:T(8,128)(2,1)}), bf16[7168,2048]{1,0:T(8,128)(2,1)}) %all-gather.4.cloned.1.call-update) | async-done | bytes 29360144 | tf_op jit(solution)/shard_map/all_gather | solution.py:40
  417.5 34.5 %reduce-scatter.4.cloned.1.call-done = bf16[256,2048]{1,0:T(8,128)(2,1)} async-done(((bf16[512,2048]{1,0:T(8,128)(2,1)}), bf16[256,2048]{1,0:T(8,128)(2,1)}) %reduce-scatter.4.cloned.1.call-update) | async-done | bytes 1048592 | tf_op jit(solution)/shard_map/reduce_scatter | solution.py:14
  452.0 130.6 %reduce-scatter.6.cloned.1.call-done = bf16[128,7168]{1,0:T(8,128)(2,1)} async-done(((bf16[512,7168]{1,0:T(8,128)(2,1)}), bf16[128,7168]{1,0:T(8,128)(2,1)}) %reduce-scatter.6.cloned.1.call-update) | async-done | bytes 1835024 | tf_op jit(solution)/shard_map/reduce_scatter | solution.py:22
  582.7 20.1 %copy.10 = bf16[7168,2048]{1,0:T(8,128)(2,1)} copy(bf16[7168,2048]{1,0:T(8,128)(2,1)} %all-gather.4.cloned.1.call-done) | data formatting | bytes 58720256
Async XLA Ops:
  8.0 216.1 %reduce-scatter.8.cloned.1.call-start = ((), (), s32[]{:S(2)}) async-start(), calls=%async_computation.5 | async-start | bytes 36700160 | tf_op jit(solution)/shard_map/reduce_scatter | solution.py:33
  8.7 255.8 %all-gather.6.cloned.1.call-start = ((), (), s32[]{:S(2)}) async-start(), calls=%async_computation.7 | async-start | bytes 3145728 | tf_op jit(solution)/shard_map/all_gather | solution.py:20
  9.3 408.2 %all-gather.4.cloned.1.call-start = ((), (), s32[]{:S(2)}) async-start(), calls=%async_computation.6 | async-start | bytes 36700160 | tf_op jit(solution)/shard_map/all_gather | solution.py:40
  239.5 212.5 %reduce-scatter.4.cloned.1.call-start = ((), (), s32[]{:S(2)}) async-start(), calls=%async_computation.3 | async-start | bytes 3145728 | tf_op jit(solution)/shard_map/reduce_scatter | solution.py:14
  264.4 318.3 %reduce-scatter.6.cloned.1.call-start = ((), (), s32[]{:S(2)}) async-start(), calls=%async_computation.4 | async-start | bytes 9175040 | tf_op jit(solution)/shard_map/reduce_scatter | solution.py:22
Sparse Core Ops, SparseCore 0:
  11.4 212.6 reduce-scatter.7
Sparse Core Ops, SparseCore 1:
  10.8 35.7 all-gather.5
  239.6 177.8 all-gather.3
  420.2 31.8 reduce-scatter.3
  454.9 127.7 reduce-scatter.5
where the time goes:
time: 610 us
  waiting for transfers between devices  511 us (84%)
  matrix products  47.9 us (8%)
  local copies, waits for them, and re-layouts  20.1 us (3%)
  between operations  15.7 us (3%)
  other arithmetic  15.4 us (3%)
    reduce_scatter x1, waiting for transfers between devices, per_device(): lax.psum_scatter(replica_terms.astype(jnp.bfloat16), 'rep', scatter_dimen...  215 us
    reduce_scatter x1, waiting for transfers between devices, per_device(): lax.psum_scatter(lax.dot_general(row_block, down_weight, (((1,), (1,)), (...  131 us
    all_gather x1, waiting for transfers between devices, per_device(): outer_step = lax.all_gather(step_share, 'rep', axis=0, tiled=True)  130 us
    reduce_scatter x1, waiting for transfers between devices, per_device(): lax.psum_scatter(jnp.dot(row_block, down_weight, preferred_element_type=j...  34.5 us
    dot_general x1, matrix products, per_device(): jnp.dot(row_block, down_weight, preferred_element_type=jnp.float32)  24.8 us
    dot_general x1, matrix products, per_device(): lax.dot_general(row_block, down_weight, (((1,), (1,)), ((), ())), preferr...  23.1 us
    unnamed x1, local copies, waits for them, and re-layouts  20.1 us
    convert_element_type x1, other arithmetic, per_device(): (outer_rate * (average + momentum_rate * new_momentum)).astype(jnp.bfloat16)  15.4 us
  transfers between devices with their start and end apart: 5, of which 4 were waited for; matrix products, arithmetic and copies ran while one was open for 10% of the time, Pallas kernels for 0%

commit v1 on v0

v1 whole, which is shorter than its diff:
```python
import functools

import jax
import jax.numpy as jnp
from jax import lax
from jax.experimental import pallas as pl
from jax.experimental.pallas import tpu as pltpu
from jax.sharding import PartitionSpec as P

outer_rate = 0.7
momentum_rate = 0.9

MESH = pl.DeviceIdType.MESH
f32 = jnp.float32
bf16 = jnp.bfloat16


def pieces(extent, unit, most):
    return max(k for k in range(1, most + 1) if extent % (k * unit) == 0)


def kernel(
    n_rep, n_dp, n_tp, n_k, n_f,
    hidden, weight, grads, pseudo, momentum,
    layer_out, hidden_grad, new_momentum, outer_step, xch,
    ps, pr, la, lb, mom, nmb, wb, hb, gf, acc, po, tr, pb, dr,
    ld_sem, xs_sem, xr_sem, ps_sem, pr_sem, ss_sem, sr_sem, fs_sem, fr_sem, own_sem,
    gs_sem, gr_sem, ts_sem, tr_sem, ds_sem, dr_sem,
):
    n_x = n_rep // 2
    rep, dp, tp = lax.axis_index("rep"), lax.axis_index("dp"), lax.axis_index("tp")
    x, core = rep // 2, lax.rem(rep, 2)
    partner = 2 * x + 1 - core
    share, cols = momentum.shape
    chunk = share // n_k
    ffn = weight.shape[0]
    fb = ffn // n_f
    tokens = hidden.shape[1]
    t_rows, d_rows = tokens // n_tp, tokens // n_dp
    row_unit = 16

    def chip(d):
        return lax.rem(x + d, n_x)

    def rep_peer(d):
        return 2 * chip(d) + core

    def rows(owner, k):
        return pl.ds(pl.multiple_of(owner * share + k * chunk, chunk), chunk)

    def part(k):
        return pl.ds(pl.multiple_of(k * chunk, chunk), chunk)

    def remote(src, dst, send, recv, axis, index):
        return pltpu.make_async_remote_copy(
            src_ref=src, dst_ref=dst, send_sem=send, recv_sem=recv,
            device_id={axis: index}, device_id_type=MESH,
        )

    def drain(ref, sem):
        pltpu.make_async_copy(ref, ref, sem).wait()

    barrier = pltpu.get_barrier_semaphore()
    peers = [("rep", partner)]
    peers += [("rep", rep_peer(d)) for d in range(1, n_x)]
    peers += [("dp", lax.rem(dp + d, n_dp)) for d in range(1, n_dp)]
    peers += [("tp", lax.rem(tp + d, n_tp)) for d in range(1, n_tp)]
    for axis, index in peers:
        pl.semaphore_signal(barrier, inc=1, device_id={axis: index}, device_id_type=MESH)
    pl.semaphore_wait(barrier, len(peers))

    def exchange(d, k):
        return remote(
            pseudo.at[0, rows(2 * chip(d) + 1 - core, k)], xch.at[d, part(k)],
            xs_sem, xr_sem.at[d, k], "rep", partner,
        )

    def start_exchange(k, carry):
        for d in range(1, n_x):
            exchange(d, k).start()
        return carry

    def start_own_exchange(k, carry):
        exchange(0, k).start()
        return carry

    lax.fori_loop(0, n_k, start_exchange, 0)

    mine = pl.ds(pl.multiple_of(tp * t_rows, t_rows), t_rows)

    def gather(d):
        return remote(grads.at[0], gf.at[mine], gs_sem.at[d - 1], gr_sem.at[d - 1],
                      "tp", lax.rem(tp + d, n_tp))

    for d in range(1, n_tp):
        gather(d).start()
    own_grads = pltpu.make_async_copy(grads.at[0], gf.at[mine], own_sem)
    own_grads.start()
    lax.fori_loop(0, n_k, start_own_exchange, 0)

    def partial_send(d, k):
        return remote(ps.at[d - 1, part(k)], pr.at[d - 1, part(k)], ps_sem,
                      pr_sem.at[d - 1, k], "rep", rep_peer(d))

    def reduce_chunk(k, carry):
        for d in range(1, n_x):
            a = pltpu.make_async_copy(pseudo.at[0, rows(rep_peer(d), k)], la, ld_sem.at[0])
            a.start()
            exchange(d, k).wait_recv()
            b = pltpu.make_async_copy(xch.at[d, part(k)], lb, ld_sem.at[1])
            b.start()
            a.wait()
            b.wait()

            def add(i, c):
                r = pl.ds(pl.multiple_of(i * row_unit, row_unit), row_unit)
                o = pl.ds(pl.multiple_of(k * chunk + i * row_unit, row_unit), row_unit)
                ps[d - 1, o, :] = (la[r, :].astype(f32) + lb[r, :].astype(f32)).astype(bf16)
                return c

            lax.fori_loop(0, chunk // row_unit, add, 0)
            partial_send(d, k).start()
        return carry

    lax.fori_loop(0, n_k, reduce_chunk, 0)

    tn = cols // pieces(cols, 128, max(1, cols // 512))
    tm = tokens // pieces(tokens, row_unit, 2)

    def clear(i, carry):
        r = pl.ds(pl.multiple_of(i * row_unit, row_unit), row_unit)
        acc[r, :] = jnp.zeros((row_unit, cols), f32)
        return carry

    lax.fori_loop(0, tokens // row_unit, clear, 0)
    own_grads.wait()
    for d in range(1, n_tp):
        gather(d).wait()

    def back_send(d, f):
        to = lax.rem(dp + d, n_dp)
        c = pl.ds(pl.multiple_of(f * fb, fb), fb)
        return remote(
            pb.at[pl.ds(pl.multiple_of(to * d_rows, d_rows), d_rows), c],
            dr.at[d - 1, :, c], ds_sem, dr_sem.at[d - 1], "dp", to,
        )

    def matmul_block(f, carry):
        c = pl.ds(pl.multiple_of(f * fb, fb), fb)
        a = pltpu.make_async_copy(weight.at[c], wb, ld_sem.at[0])
        b = pltpu.make_async_copy(hidden.at[0, :, c], hb, ld_sem.at[1])
        a.start()
        b.start()
        a.wait()
        b.wait()

        def back(m, z):
            r = pl.ds(pl.multiple_of(m * tm, tm), tm)
            product = lax.dot_general(
                gf[r, :], wb[...], (((1,), (1,)), ((), ())), preferred_element_type=f32
            )
            pb[r, c] = product.astype(bf16)
            return z

        lax.fori_loop(0, tokens // tm, back, 0)
        for d in range(1, n_dp):
            back_send(d, f).start()

        def forward(n, z):
            t = pl.ds(pl.multiple_of(n * tn, tn), tn)
            acc[:, t] += jnp.dot(hb[...], wb[:, t], preferred_element_type=f32)
            return z

        lax.fori_loop(0, cols // tn, forward, 0)
        return carry

    lax.fori_loop(0, n_f, matmul_block, 0)

    def round_out(i, carry):
        r = pl.ds(pl.multiple_of(i * row_unit, row_unit), row_unit)
        po[r, :] = acc[r, :].astype(bf16)
        return carry

    lax.fori_loop(0, tokens // row_unit, round_out, 0)

    def out_send(d):
        to = lax.rem(tp + d, n_tp)
        return remote(po.at[pl.ds(pl.multiple_of(to * t_rows, t_rows), t_rows)],
                      tr.at[d - 1], ts_sem.at[d - 1], tr_sem.at[d - 1], "tp", to)

    for d in range(1, n_tp):
        out_send(d).start()

    def store_momentum(k):
        return pltpu.make_async_copy(nmb, new_momentum.at[part(k)], ld_sem.at[3])

    def step_send(d, k):
        return remote(pr.at[0, part(k)], outer_step.at[rows(rep, k)], ss_sem,
                      sr_sem.at[d - 1, k], "rep", rep_peer(d))

    def update_chunk(k, carry):
        a = pltpu.make_async_copy(pseudo.at[0, rows(rep, k)], la, ld_sem.at[0])
        m = pltpu.make_async_copy(momentum.at[part(k)], mom, ld_sem.at[2])
        a.start()
        m.start()
        exchange(0, k).wait_recv()
        b = pltpu.make_async_copy(xch.at[0, part(k)], lb, ld_sem.at[1])
        b.start()
        for d in range(1, n_x):
            partial_send(d, k).wait_recv()

        @pl.when(k > 0)
        def _():
            store_momentum(k - 1).wait()

        a.wait()
        b.wait()
        m.wait()

        def update(i, c):
            r = pl.ds(pl.multiple_of(i * row_unit, row_unit), row_unit)
            o = pl.ds(pl.multiple_of(k * chunk + i * row_unit, row_unit), row_unit)
            total = la[r, :].astype(f32) + lb[r, :].astype(f32)
            for d in range(1, n_x):
                total += pr[d - 1, o, :].astype(f32)
            average = total / n_rep
            fresh = momentum_rate * mom[r, :] + average
            nmb[r, :] = fresh
            pr[0, o, :] = (outer_rate * (average + momentum_rate * fresh)).astype(bf16)
            return c

        lax.fori_loop(0, chunk // row_unit, update, 0)
        for d in range(1, n_x):
            step_send(d, k).start()
        remote(pr.at[0, part(k)], outer_step.at[rows(rep, k)], fs_sem, fr_sem,
               "rep", partner).start()
        pltpu.make_async_copy(pr.at[0, part(k)], outer_step.at[rows(rep, k)], own_sem).start()
        store_momentum(k).start()
        return carry

    lax.fori_loop(0, n_k, update_chunk, 0)
    store_momentum(n_k - 1).wait()

    def forward_chunk(k, carry):
        for d in range(1, n_x):
            step_send(d, k).wait_recv()
            r = rows(2 * chip(n_x - d) + core, k)
            remote(outer_step.at[r], outer_step.at[r], fs_sem, fr_sem, "rep", partner).start()
        return carry

    lax.fori_loop(0, n_k // 2, forward_chunk, 0)

    for d in range(1, n_tp):
        out_send(d).wait()

    def sum_out(i, carry):
        r = pl.ds(pl.multiple_of(i * row_unit, row_unit), row_unit)
        o = pl.ds(pl.multiple_of(tp * t_rows + i * row_unit, row_unit), row_unit)
        total = po[o, :].astype(f32)
        for d in range(1, n_tp):
            total += tr[d - 1, r, :].astype(f32)
        tr[0, r, :] = total.astype(bf16)
        return carry

    lax.fori_loop(0, t_rows // row_unit, sum_out, 0)
    out_copy = pltpu.make_async_copy(tr.at[0], layer_out.at[0], ld_sem.at[0])
    out_copy.start()

    for d in range(1, n_dp):
        drain(dr.at[d - 1], dr_sem.at[d - 1])

    def sum_back(f, carry):
        c = pl.ds(pl.multiple_of(f * fb, fb), fb)

        def band(i, z):
            r = pl.ds(pl.multiple_of(i * row_unit, row_unit), row_unit)
            o = pl.ds(pl.multiple_of(dp * d_rows + i * row_unit, row_unit), row_unit)
            total = pb[o, c].astype(f32)
            for d in range(1, n_dp):
                total += dr[d - 1, r, c].astype(f32)
            dr[0, r, c] = total.astype(bf16)
            return z

        lax.fori_loop(0, d_rows // row_unit, band, 0)
        return carry

    lax.fori_loop(0, n_f, sum_back, 0)
    back_copy = pltpu.make_async_copy(dr.at[0], hidden_grad.at[0], ld_sem.at[1])
    back_copy.start()

    lax.fori_loop(n_k // 2, n_k, forward_chunk, 0)

    out_copy.wait()
    back_copy.wait()
    drain(xch, xs_sem)
    drain(ps, ps_sem)
    drain(ps, ss_sem)
    drain(xch, fs_sem)
    drain(xch, fr_sem)
    drain(pr.at[0], own_sem)
    drain(dr, ds_sem)


def per_device(sizes, hidden, down_weight, out_grad, pseudo_grad, momentum):
    n_rep, n_dp, n_tp = sizes
    n_x = n_rep // 2
    tokens = hidden.shape[1]
    ffn, cols = down_weight.shape
    share = momentum.shape[0]
    n_k = pieces(share, 16, 14)
    n_f = pieces(ffn, 128, 14)
    chunk, fb = share // n_k, ffn // n_f
    t_rows, d_rows = tokens // n_tp, tokens // n_dp
    dma = pltpu.SemaphoreType.DMA
    out = pl.pallas_call(
        functools.partial(kernel, n_rep, n_dp, n_tp, n_k, n_f),
        out_shape=(
            jax.ShapeDtypeStruct((1, t_rows, cols), bf16),
            jax.ShapeDtypeStruct((1, d_rows, ffn), bf16),
            jax.ShapeDtypeStruct((share, cols), f32),
            jax.ShapeDtypeStruct((ffn, cols), bf16),
            jax.ShapeDtypeStruct((n_x, share, cols), bf16),
        ),
        in_specs=[pl.BlockSpec(memory_space=pl.ANY)] * 5,
        out_specs=[pl.BlockSpec(memory_space=pl.ANY)] * 5,
        scratch_shapes=[
            pltpu.VMEM((n_x - 1, share, cols), bf16),
            pltpu.VMEM((n_x - 1, share, cols), bf16),
            pltpu.VMEM((chunk, cols), bf16),
            pltpu.VMEM((chunk, cols), bf16),
            pltpu.VMEM((chunk, cols), f32),
            pltpu.VMEM((chunk, cols), f32),
            pltpu.VMEM((fb, cols), bf16),
            pltpu.VMEM((tokens, fb), bf16),
            pltpu.VMEM((tokens, cols), bf16),
            pltpu.VMEM((tokens, cols), f32),
            pltpu.VMEM((tokens, cols), bf16),
            pltpu.VMEM((n_tp - 1, t_rows, cols), bf16),
            pltpu.VMEM((tokens, ffn), bf16),
            pltpu.VMEM((n_dp - 1, d_rows, ffn), bf16),
            dma((4,)),
            dma,
            dma((n_x, n_k)),
            dma,
            dma((n_x - 1, n_k)),
            dma,
            dma((n_x - 1, n_k)),
            dma,
            dma,
            dma,
            dma((n_tp - 1,)),
            dma((n_tp - 1,)),
            dma((n_tp - 1,)),
            dma((n_tp - 1,)),
            dma,
            dma((n_dp - 1,)),
        ],
        compiler_params=pltpu.CompilerParams(
            collective_id=0, has_side_effects=True, vmem_limit_bytes=60 * 2**20
        ),
        name="layer_step",
    )(hidden, down_weight, out_grad, pseudo_grad, momentum)
    return out[:4]


def solution(mesh):
    sizes = tuple(mesh.shape[a] for a in ("rep", "dp", "tp"))
    return jax.shard_map(
        functools.partial(per_device, sizes),
        mesh=mesh,
        in_specs=(
            P("rep", None, "tp"),
            P("tp", "dp"),
            P("rep", "tp", "dp"),
            P("rep", "tp", "dp"),
            P(("tp", "rep"), "dp"),
        ),
        out_specs=(
            P("rep", "tp", "dp"),
            P("rep", "dp", "tp"),
            P(("tp", "rep"), "dp"),
            P("tp", "dp"),
        ),
        check_vma=False,
    )
```

time: 610 us -> 368 us (0.60)
  waiting for transfers between devices: 511 us -> 0 us
  Pallas kernels: 0 us -> 328 us
  matrix products: 47.9 us -> 0 us
  local copies, waits for them, and re-layouts: 20.1 us -> 38.6 us
  other arithmetic: 15.4 us -> 0 us
  between operations: 15.7 us -> 0.64 us
    reduce_scatter x3 -> x0, waiting for transfers between devices: 380 us -> none  [the longest x1 215 us: per_device(): lax.psum_scatter(replica_terms.astype(jnp.bfloat16), 'rep', scatter_dimen...]
    pallas_call x0 -> x1, Pallas kernels: none -> 328 us  [per_device(): pl.pallas_call(functools.partial(kernel, n_rep, n_dp, n_tp, n_k, n_f), ou...]
    all_gather x2 -> x0, waiting for transfers between devices: 130 us -> none  [the longest x1 130 us: per_device(): outer_step = lax.all_gather(step_share, 'rep', axis=0, tiled=True)]
    dot_general x2 -> x0, matrix products: 47.9 us -> none  [the longest x1 24.8 us: per_device(): jnp.dot(row_block, down_weight, preferred_element_type=jnp.float32)]
    unnamed x1 -> x4, local copies, waits for them, and re-layouts: 20.1 us -> 38.6 us
    convert_element_type x1 -> x0, other arithmetic: 15.4 us -> none  [per_device(): (outer_rate * (average + momentum_rate * new_momentum)).astype(jnp.bfloat16)]
  transfers between devices with their start and end apart: 5 -> 0, of which waited for: 4 -> 0; matrix products, arithmetic and copies ran while one was open for 10% -> 0% of each run, Pallas kernels for 0% -> 0%
where the time goes in v1:
time: 368 us; the launch traced here: 367 us
  Pallas kernels  328 us (89%)
  local copies, waits for them, and re-layouts  38.6 us (10%)
    pallas_call x1, Pallas kernels, per_device(): pl.pallas_call(functools.partial(kernel, n_rep, n_dp, n_tp, n_k, n_f), ou...  328 us
    unnamed x4, local copies, waits for them, and re-layouts  38.6 us

profile of v1, /device:TPU:0, one launch (start us, length us, event | category | flops | bytes accessed | tf_op | source)
XLA Modules:
  0.0 366.9 jit_solution(13719585557110484228)
XLA Ops:
  0.6 327.7 %layer_step.1 = (bf16[1,256,2048]{2,1,0:T(8,128)(2,1)}, bf16[1,128,7168]{2,1,0:T(8,128)(2,1)}, f32[1792,2048]{1,0:T(8,128)}, bf16[7168,2048]{1,0:T(8,128)(2,1)}, bf16[2,1792,2048]{2,1,0:T(8,128)(2,1)}) custom-call(bf16[1,512,7168]{2,1,0:T(8,128)(2,1)} %hidden.1, bf16[7168,2048]{1,0:T(8,128)(2,1)} %weight.1, bf16[1,256,2048]{2,1,0:T(8,128)(2,1)} %grads.1, ...), custom_call_target="tpu_custom_call" | custom-call | tf_op jit(solution)/shard_map/layer_step/pallas_call | solution.py:315
  328.3 2.3 copy.13
  330.6 2.8 copy.14
  333.5 13.4 %copy.15 = f32[1792,2048]{1,0:T(8,128)} copy(f32[1792,2048]{1,0:T(8,128)} %get-tuple-element.18) | data formatting | bytes 29360128
  346.8 20.1 %copy.16 = bf16[7168,2048]{1,0:T(8,128)(2,1)} copy(bf16[7168,2048]{1,0:T(8,128)(2,1)} %get-tuple-element.19) | data formatting | bytes 58720256

commit v2 on v1

--- a/solution.py
+++ b/solution.py
@@ -20,9 +20,9 @@
 
 
 def kernel(
-    n_rep, n_dp, n_tp, n_k, n_f,
+    n_rep, n_dp, n_tp, n_k, n_late, n_f,
     hidden, weight, grads, pseudo, momentum,
-    layer_out, hidden_grad, new_momentum, outer_step, xch,
+    layer_out, hidden_grad, new_momentum, outer_step, late, xch,
     ps, pr, la, lb, mom, nmb, wb, hb, gf, acc, po, tr, pb, dr,
     ld_sem, xs_sem, xr_sem, ps_sem, pr_sem, ss_sem, sr_sem, fs_sem, fr_sem, own_sem,
     gs_sem, gr_sem, ts_sem, tr_sem, ds_sem, dr_sem,
@@ -38,6 +38,8 @@
     tokens = hidden.shape[1]
     t_rows, d_rows = tokens // n_tp, tokens // n_dp
     row_unit = 16
+    n_sent = n_k - n_late
+    sent = pl.ds(0, n_sent * chunk)
 
     def chip(d):
         return lax.rem(x + d, n_x)
@@ -230,16 +232,26 @@
             return c
 
         lax.fori_loop(0, chunk // row_unit, update, 0)
-        for d in range(1, n_x):
-            step_send(d, k).start()
-        remote(pr.at[0, part(k)], outer_step.at[rows(rep, k)], fs_sem, fr_sem,
-               "rep", partner).start()
-        pltpu.make_async_copy(pr.at[0, part(k)], outer_step.at[rows(rep, k)], own_sem).start()
+
+        @pl.when(k < n_sent)
+        def _():
+            for d in range(1, n_x):
+                step_send(d, k).start()
+            remote(pr.at[0, part(k)], outer_step.at[rows(rep, k)], fs_sem, fr_sem,
+                   "rep", partner).start()
+            pltpu.make_async_copy(
+                pr.at[0, part(k)], outer_step.at[rows(rep, k)], own_sem
+            ).start()
+
         store_momentum(k).start()
         return carry
 
     lax.fori_loop(0, n_k, update_chunk, 0)
     store_momentum(n_k - 1).wait()
+    late_copy = pltpu.make_async_copy(
+        pr.at[0, pl.ds(n_sent * chunk, n_late * chunk)], late, ld_sem.at[3]
+    )
+    late_copy.start()
 
     def forward_chunk(k, carry):
         for d in range(1, n_x):
@@ -248,7 +260,7 @@
             remote(outer_step.at[r], outer_step.at[r], fs_sem, fr_sem, "rep", partner).start()
         return carry
 
-    lax.fori_loop(0, n_k // 2, forward_chunk, 0)
+    lax.fori_loop(0, n_sent // 2, forward_chunk, 0)
 
     for d in range(1, n_tp):
         out_send(d).wait()
@@ -288,17 +300,24 @@
     back_copy = pltpu.make_async_copy(dr.at[0], hidden_grad.at[0], ld_sem.at[1])
     back_copy.start()
 
-    lax.fori_loop(n_k // 2, n_k, forward_chunk, 0)
+    lax.fori_loop(n_sent // 2, n_sent, forward_chunk, 0)
 
     out_copy.wait()
     back_copy.wait()
+    late_copy.wait()
     drain(xch, xs_sem)
     drain(ps, ps_sem)
-    drain(ps, ss_sem)
-    drain(xch, fs_sem)
-    drain(xch, fr_sem)
-    drain(pr.at[0], own_sem)
+    drain(ps.at[:, sent], ss_sem)
+    drain(xch.at[:, sent], fs_sem)
+    drain(xch.at[:, sent], fr_sem)
+    drain(pr.at[0, sent], own_sem)
     drain(dr, ds_sem)
+
+
+def copy_bands(*refs):
+    half = len(refs) // 2
+    for source, target in zip(refs[:half], refs[half:]):
+        target[...] = source[...]
 
 
 def per_device(sizes, hidden, down_weight, out_grad, pseudo_grad, momentum):
@@ -309,20 +328,23 @@
     share = momentum.shape[0]
     n_k = pieces(share, 16, 14)
     n_f = pieces(ffn, 128, 14)
+    n_late = max(1, n_k // 7)
     chunk, fb = share // n_k, ffn // n_f
+    late_rows = n_late * chunk
     t_rows, d_rows = tokens // n_tp, tokens // n_dp
     dma = pltpu.SemaphoreType.DMA
     out = pl.pallas_call(
-        functools.partial(kernel, n_rep, n_dp, n_tp, n_k, n_f),
+        functools.partial(kernel, n_rep, n_dp, n_tp, n_k, n_late, n_f),
         out_shape=(
             jax.ShapeDtypeStruct((1, t_rows, cols), bf16),
             jax.ShapeDtypeStruct((1, d_rows, ffn), bf16),
             jax.ShapeDtypeStruct((share, cols), f32),
             jax.ShapeDtypeStruct((ffn, cols), bf16),
+            jax.ShapeDtypeStruct((late_rows, cols), bf16),
             jax.ShapeDtypeStruct((n_x, share, cols), bf16),
         ),
         in_specs=[pl.BlockSpec(memory_space=pl.ANY)] * 5,
-        out_specs=[pl.BlockSpec(memory_space=pl.ANY)] * 5,
+        out_specs=[pl.BlockSpec(memory_space=pl.ANY)] * 6,
         scratch_shapes=[
             pltpu.VMEM((n_x - 1, share, cols), bf16),
             pltpu.VMEM((n_x - 1, share, cols), bf16),
@@ -360,7 +382,34 @@
         ),
         name="layer_step",
     )(hidden, down_weight, out_grad, pseudo_grad, momentum)
-    return out[:4]
+    layer_out, hidden_grad, new_momentum, outer_step, late = out[:5]
+    late = lax.all_gather(late, "rep", axis=0, tiled=False)
+    results = (layer_out, hidden_grad, new_momentum, outer_step)
+    steps = max(
+        k for k in range(1, 9)
+        if not any(n % (16 * k) for n in (t_rows, d_rows, ffn)) and share % (8 * k) == 0
+    )
+
+    def band(array):
+        block = array.shape[:-2] + (array.shape[-2] // steps, array.shape[-1])
+        return pl.BlockSpec(block, lambda i: (0,) * (array.ndim - 2) + (i, 0))
+
+    layer_out, hidden_grad, new_momentum, outer_step = pl.pallas_call(
+        copy_bands,
+        out_shape=tuple(jax.ShapeDtypeStruct(r.shape, r.dtype) for r in results),
+        grid=(steps,),
+        in_specs=[band(r) for r in results],
+        out_specs=[band(r) for r in results],
+        cost_estimate=pl.CostEstimate(
+            flops=0, bytes_accessed=2 * sum(r.nbytes for r in results), transcendentals=0
+        ),
+        compiler_params=pltpu.CompilerParams(vmem_limit_bytes=40 * 2**20),
+        name="result_copy",
+    )(*results)
+    outer_step = lax.dynamic_update_slice(
+        outer_step.reshape(n_rep, share, cols), late, (0, share - late_rows, 0)
+    ).reshape(ffn, cols)
+    return layer_out, hidden_grad, new_momentum, outer_step
 
 
 def solution(mesh):

time: 368 us -> 359 us (0.976)
  local copies, waits for them, and re-layouts: 38.6 us -> 7.5 us
  between operations: 0.64 us -> 14 us
  Pallas kernels: 328 us -> 335 us
    unnamed x4, local copies, waits for them, and re-layouts: 38.6 us -> 2.72 us
    pallas_call x1 -> x2, Pallas kernels: 328 us -> 335 us  [the longest x1 305 us: per_device(): pl.pallas_call(functools.partial(kernel, n_rep, n_dp, n_tp, n_k, n_late,...]
    dynamic_update_slice x0 -> x1, local copies, waits for them, and re-layouts: none -> 4.79 us  [per_device(): lax.dynamic_update_slice(outer_step.reshape(n_rep, share, cols), late, (0...]
  transfers between devices with their start and end apart: 0 -> 1, of which waited for: 0 -> 0; matrix products, arithmetic and copies ran while one was open for 0% -> 0% of each run, Pallas kernels for 0% -> 8%
where the time goes in v2:
time: 359 us; the launch traced here: 357 us
  Pallas kernels  335 us (93%)
  between operations  14 us (4%)
  local copies, waits for them, and re-layouts  7.5 us (2%)
    pallas_call x1, Pallas kernels, per_device(): pl.pallas_call(functools.partial(kernel, n_rep, n_dp, n_tp, n_k, n_late,...  305 us
    pallas_call x1, Pallas kernels, per_device(): pl.pallas_call(copy_bands, out_shape=tuple((jax.ShapeDtypeStruct(r.shape,...  30.3 us
  transfers between devices with their start and end apart: 1, of which 0 were waited for; matrix products, arithmetic and copies ran while one was open for 0% of the time, Pallas kernels for 8%

profile of v2, /device:TPU:0, one launch (start us, length us, event | category | flops | bytes accessed | tf_op | source)
XLA Modules:
  0.0 357.1 jit_solution(11183170394897782424)
XLA Ops:
  7.2 0.0 all-gather.3.cloned.1.call-start
  7.2 305.2 %layer_step.1 = (bf16[1,256,2048]{2,1,0:T(8,128)(2,1)}, bf16[1,128,7168]{2,1,0:T(8,128)(2,1)}, f32[1792,2048]{1,0:T(8,128)}, bf16[7168,2048]{1,0:T(8,128)(2,1)},...) custom-call(bf16[1,512,7168]{2,1,0:T(8,128)(2,1)} %hidden.1, bf16[7168,2048]{1,0:T(8,128)(2,1)} %weight.1, ...), custom_call_target="tpu_custom_call" | custom-call | tf_op jit(solution)/shard_map/layer_step/pallas_call | solution.py:336
  312.4 0.0 all-gather.3.cloned.1.call-update
  312.5 0.0 copy-start
  312.5 1.5 copy-done
  314.0 0.0 copy-start.1
  314.0 1.2 copy-done.1
  315.2 30.3 %result_copy.1 = (bf16[1,256,2048]{2,1,0:T(8,128)(2,1)}, bf16[1,128,7168]{2,1,0:T(8,128)(2,1)}, f32[1792,2048]{1,0:T(8,128)}, bf16[7168,2048]{1,0:T(8,128)(2,1)}) custom-call(bf16[1,256,2048]{2,1,0:T(8,128)(2,1)S(1)} %copy-done.1, bf16[1,128,7168]{2,1,0:T(8,128)(2,1)S(1)} %copy-done, f32[1792,2048]{1,0:T(8,128)} %get-tuple-element.15.refs_2_, ...), custom_call_target="tpu_custom_call" | custom-call | bytes 93847552 | tf_op jit(solution)/shard_map/result_copy/pallas_call | solution.py:397
  345.4 0.0 all-gather.3.cloned.1.call-done
  345.4 4.8 %constant_dynamic-update-slice_fusion = bf16[4,1792,2048]{2,1,0:T(8,128)(2,1)} fusion(bf16[4,1792,2048]{2,1,0:T(8,128)(2,1)} %bitcast.4, bf16[4,256,2048]{2,1,0:T(8,128)(2,1)} %bitcast.3), kind=kLoop, calls=%fused_computation | loop fusion | bytes 8388608 | tf_op jit(solution)/shard_map/dynamic_update_slice | solution.py:409
Async XLA Ops:
  7.2 338.3 %all-gather.3.cloned.1.call-start = ((), (), s32[]{:S(2)}) async-start(), calls=%async_computation | async-start | bytes 5242880 | tf_op jit(solution)/shard_map/all_gather | solution.py:386
  312.5 1.5 copy-start
  314.0 1.2 copy-start.1
Sparse Core Ops, SparseCore 0:
  312.6 32.6 all-gather.2
